TPU v7x, 32 devices: a whole 2x2x4 slice. The times are simulated.
32 devices in a mesh: mem: 4 (over x, core), tile: 8 (over z, y).
Axes of the slice: x: 2, y: 2, z: 4, core: 2. Of those that a mesh axis runs over, the one named last changes fastest.
Arguments:
- alpha: bfloat16 [80, 64, 32, 128], P('mem', 'tile'), may hold values from -0.8984375 to 0.8984375
- ensemble: bfloat16 [80, 3, 64, 32, 128], P('mem', None, 'tile'), may hold values from -6 to 6
- loc_vert: bfloat16 [128, 128], replicated, may hold values from -0.25 to 1.5, as said below
- obs_col: int32 [8, 2048], P('tile'), may hold values from 0 to 1023
- obs_lev: int32 [8, 2048], P('tile'), may hold values from 0 to 127
- obs_count: int32 [8], P('tile'), may hold values from 512 to 2048
- innovation: float32 [8, 2048], P('tile'), may hold values from -6 to 6
- obs_weight: float32 [8, 2048], P('tile'), may hold values from 1 to 8
Outputs:
- gradient: float32 [80, 64, 32, 128], P('mem', 'tile')
Inputs may be any that keep to these rules, and one draw needn't show every extreme that they name: `loc_vert`: a square root of the vertical localization, applied along levels.
All inputs are finite; a program needn't handle non-finite values.
Results may differ from a plain program's by a relative error of at most 0.0019.
Values sent between devices are 32-bit elements; how exact they have to be, the bound alone decides.
A program may use at most 64 MiB of HBM per device.

v0:
```python
import jax
import jax.numpy as jnp
from jax import lax
from jax.sharding import PartitionSpec as P

V = 3
NS = 2


def padded_2(block, sides, width):
    for axis, dim in sides:
        count = lax.axis_size(axis)
        forward = [(i, i + 1) for i in range(count - 1)]
        backward = [(target, source) for source, target in forward]
        low = lax.ppermute(
            lax.slice_in_dim(block, block.shape[dim] - width, None, axis=dim), axis, forward
        )
        high = lax.ppermute(lax.slice_in_dim(block, 0, width, axis=dim), axis, backward)
        block = jnp.concatenate([low, block, high], axis=dim)
    return block


def widen(field, axis):
    pads = [(1, 1) if dim == axis else (0, 0) for dim in range(field.ndim)]
    return jnp.pad(field, pads)


def spread(padded, axis):
    length = padded.shape[axis] - 2
    before = lax.slice_in_dim(padded, 0, length, axis=axis)
    middle = lax.slice_in_dim(padded, 1, length + 1, axis=axis)
    after = lax.slice_in_dim(padded, 2, length + 2, axis=axis)
    return 0.25 * before + 0.5 * middle + 0.25 * after


def refine(padded, axis):
    length = padded.shape[axis] - 2
    before = lax.slice_in_dim(padded, 0, length, axis=axis)
    middle = lax.slice_in_dim(padded, 1, length + 1, axis=axis)
    after = lax.slice_in_dim(padded, 2, length + 2, axis=axis)
    evens = 0.75 * middle + 0.25 * before
    odds = 0.75 * middle + 0.25 * after
    stacked = jnp.stack([evens, odds], axis=axis + 1)
    shape = list(middle.shape)
    shape[axis] = 2 * length
    return stacked.reshape(shape)


def coarsen(padded, axis):
    length = padded.shape[axis] - 2
    first = lax.slice_in_dim(padded, 0, length, 2, axis=axis)
    second = lax.slice_in_dim(padded, 1, length + 1, 2, axis=axis)
    third = lax.slice_in_dim(padded, 2, length + 2, 2, axis=axis)
    fourth = lax.slice_in_dim(padded, 3, length + 2, 2, axis=axis)
    return 0.25 * first + 0.75 * second + 0.75 * third + 0.25 * fourth


def smooth(field, forward):
    rows = field.shape[1]
    if forward:
        padded = padded_2(field, (("tile", 1),), NS)
    else:
        padded = padded_2(field, (("tile", 1),), NS)
    global_row = lax.axis_index("tile") * rows - NS + jnp.arange(rows + 2 * NS, dtype=jnp.int32)
    inside = (global_row >= 0) & (global_row < rows * lax.axis_size("tile"))
    for sweep in range(NS):
        padded = spread(widen(padded, 1), 1)
        padded = spread(widen(padded, 2), 2)
        padded = jnp.where(inside[None, :, None, None], padded, jnp.zeros_like(padded))
    return padded[:, NS : NS + rows]


def on_device(alpha, ensemble, loc_vert, obs_col, obs_lev, obs_count, innovation, obs_weight):
    lifted = smooth(jnp.dot(alpha, loc_vert.T, preferred_element_type=jnp.float32), True).astype(
        jnp.bfloat16
    )
    partial_inc = jnp.einsum(
        "kvyxl,kyxl->vyxl", ensemble, lifted, preferred_element_type=jnp.float32
    )
    increment = lax.psum(partial_inc, "mem")
    padded = padded_2(increment, (("tile", 1),), 1)
    fine = refine(widen(refine(padded, 1), 2), 2)
    fine_rows = fine.shape[1]
    fine_cols = fine.shape[2]
    share = fine.shape[3]
    flat = fine.reshape(V, fine_rows * fine_cols, share)
    column = obs_col[0]
    level = obs_lev[0]
    slots = column.shape[0]
    variable = jnp.arange(slots, dtype=jnp.int32) % V
    level_hot = (level[:, None] == jnp.arange(share, dtype=jnp.int32)[None, :]).astype(jnp.float32)
    picked = flat[variable, column]
    value = jnp.sum(picked * level_hot, axis=1)
    live = jnp.arange(slots, dtype=jnp.int32) < obs_count[0]
    weighted = jnp.where(live, obs_weight[0] * (value - innovation[0]), jnp.zeros_like(value))
    spread_back = weighted[:, None] * level_hot
    fine_adjoint = (
        jnp.zeros((V, fine_rows * fine_cols, share), jnp.float32)
        .at[variable, column]
        .add(spread_back)
    )
    fine_adjoint = fine_adjoint.reshape(V, fine_rows, fine_cols, share)
    fine_padded = padded_2(fine_adjoint, (("tile", 1),), 1)
    coarse_adjoint = coarsen(widen(coarsen(fine_padded, 1), 2), 2)
    back = jnp.einsum("kvyxl,vyxl->kyxl", ensemble.astype(jnp.float32), coarse_adjoint)
    back = smooth(back, False)
    return alpha.astype(jnp.float32) + jnp.dot(
        back, loc_vert.astype(jnp.float32), precision=lax.Precision.HIGHEST
    )


def solution(mesh):
    in_specs = (
        P("mem", "tile", None, None),
        P("mem", None, "tile", None, None),
        P(),
        P("tile", None),
        P("tile", None),
        P("tile"),
        P("tile", None),
        P("tile", None),
    )
    out_specs = P("mem", "tile", None, None)
    return jax.shard_map(
        on_device, mesh=mesh, in_specs=in_specs, out_specs=out_specs, check_vma=False
    )
```

profile of v0, /device:TPU:12, one launch (start us, length us, event | category | flops | bytes accessed | tf_op | source)
XLA Modules:
  0.0 186.1 jit_solution(4356748677791555464)
XLA Ops:
  7.3 1.8 fusion.62
  10.1 3.4 %collective-permute-start = (f32[20,2,32,128]{3,2,1,0:T(8,128)}, f32[20,2,32,128]{3,2,1,0:T(8,128)}, u32[]{:S(2)}, u32[]{:S(2)}) collective-permute-start(f32[20,2,32,128]{3,2,1,0:T(8,128)} %get-tuple-element.11), channel_id=1, source_target_pairs={{0,1},{1,2},{2,3},{3,4},{4,5},{5,6},{6,7},{8,9},{9,10},{10,11},{11... | collective-permute-start | bytes 1966088 | tf_op jit(solution)/shard_map/ppermute | solution.py:15
  13.5 2.4 %collective-permute-start.1 = (f32[20,2,32,128]{3,2,1,0:T(8,128)S(1)}, f32[20,2,32,128]{3,2,1,0:T(8,128)}, u32[]{:S(2)}, u32[]{:S(2)}) collective-permute-start(f32[20,2,32,128]{3,2,1,0:T(8,128)S(1)} %get-tuple-element.12), channel_id=1, source_target_pairs={{1,0},{2,1},{3,2},{4,3},{5,4},{6,5},{7,6},{9,8},{10,9},{11,10},{12... | collective-permute-start | bytes 1966088 | tf_op jit(solution)/shard_map/ppermute | solution.py:18
  16.1 26.7 %collective-permute-done = f32[20,2,32,128]{3,2,1,0:T(8,128)} collective-permute-done((f32[20,2,32,128]{3,2,1,0:T(8,128)}, f32[20,2,32,128]{3,2,1,0:T(8,128)}, u32[]{:S(2)}, u32[]{:S(2)}) %collective-permute-start) | collective-permute-done | bytes 655392 | tf_op jit(solution)/shard_map/ppermute | solution.py:15
  42.8 1.7 pad_maximum_fusion
  47.3 1.5 pad_slice_fusion.5
  51.0 1.7 multiply_reduce_fusion.1
  52.9 33.8 %all-reduce.12.cloned.1.call-done = f32[3,8,32,128]{3,2,1,0:T(8,128)} async-done(((f32[3,8,32,128]{3,2,1,0:T(8,128)}), f32[3,8,32,128]{3,2,1,0:T(8,128)}) %all-reduce.12.cloned.1.call-update) | async-done | bytes 393232 | tf_op jit(solution)/shard_map/psum | solution.py:80
  87.6 3.4 %collective-permute-start.2 = (f32[3,1,32,128]{3,2,1,0:T(8,128)S(1)}, f32[3,1,32,128]{3,2,1,0:T(8,128)S(1)}, u32[]{:S(2)}, u32[]{:S(2)}) collective-permute-start(f32[3,1,32,128]{3,2,1,0:T(8,128)S(1)} %get-tuple-element.19), channel_id=1, source_target_pairs={{0,1},{1,2},{2,3},{3,4},{4,5},{5,6},{6,7},{8,9},{9,10},{10,11},{11... | collective-permute-start | bytes 147464 | tf_op jit(solution)/shard_map/ppermute | solution.py:15
  90.9 2.6 %collective-permute-start.3 = (f32[3,1,32,128]{3,2,1,0:T(8,128)S(1)}, f32[3,1,32,128]{3,2,1,0:T(8,128)S(1)}, u32[]{:S(2)}, u32[]{:S(2)}) collective-permute-start(f32[3,1,32,128]{3,2,1,0:T(8,128)S(1)} %get-tuple-element.20), channel_id=1, source_target_pairs={{1,0},{2,1},{3,2},{4,3},{5,4},{6,5},{7,6},{9,8},{10,9},{11,10},{12... | collective-permute-start | bytes 147464 | tf_op jit(solution)/shard_map/ppermute | solution.py:18
  94.3 3.6 %collective-permute-done.3 = f32[3,1,32,128]{3,2,1,0:T(8,128)S(1)} collective-permute-done((f32[3,1,32,128]{3,2,1,0:T(8,128)S(1)}, f32[3,1,32,128]{3,2,1,0:T(8,128)S(1)}, u32[]{:S(2)}, u32[]{:S(2)}) %collective-permute-start.3) | collective-permute-done | bytes 49184 | tf_op jit(solution)/shard_map/ppermute | solution.py:18
  97.8 1.4 fusion.60
  99.5 1.5 pad_maximum_fusion.3
  101.1 13.0 %gather_fusion = f32[2048,128]{1,0:T(8,128)S(1)} fusion(f32[3,1024,128]{2,1,0:T(8,128)S(1)} %bitcast.41, s32[2048]{0:T(1024)S(1)} %bitcast.40), kind=kCustom, calls=%fused_computation | custom fusion | bytes 2113536 | tf_op jit(solution)/shard_map/gather | solution.py:92
  114.8 13.1 %scatter_custom_fusion = f32[3072,128]{1,0:T(8,128)S(1)} fusion(s32[2048]{0:T(1024)S(1)} %broadcast_select_fusion, f32[]{:T(128)} %constant.16.clone.1, f32[2048]{0:T(1024)S(1)} %multiply_select_fusion, s32[2048]{0:T(1024)S(1)} %bitcast.52), kind=kCustom, calls=%fused_computation.70 | custom fusion | flops 786432 | bytes 1590272
  128.0 2.5 %collective-permute-start.4 = (f32[3,1,64,128]{3,2,1,0:T(8,128)S(1)}, f32[3,1,64,128]{3,2,1,0:T(8,128)S(1)}, u32[]{:S(2)}, u32[]{:S(2)}) collective-permute-start(f32[3,1,64,128]{3,2,1,0:T(8,128)S(1)} %get-tuple-element.13), channel_id=1, source_target_pairs={{0,1},{1,2},{2,3},{3,4},{4,5},{5,6},{6,7},{8,9},{9,10},{10,11},{11... | collective-permute-start | bytes 294920 | tf_op jit(solution)/shard_map/ppermute | solution.py:15
  130.5 3.4 %collective-permute-start.5 = (f32[3,1,64,128]{3,2,1,0:T(8,128)S(1)}, f32[3,1,64,128]{3,2,1,0:T(8,128)S(1)}, u32[]{:S(2)}, u32[]{:S(2)}) collective-permute-start(f32[3,1,64,128]{3,2,1,0:T(8,128)S(1)} %get-tuple-element.14), channel_id=1, source_target_pairs={{1,0},{2,1},{3,2},{4,3},{5,4},{6,5},{7,6},{9,8},{10,9},{11,10},{12... | collective-permute-start | bytes 294920 | tf_op jit(solution)/shard_map/ppermute | solution.py:18
  133.9 1.7 collective-permute-done.4
  135.5 2.4 %collective-permute-done.5 = f32[3,1,64,128]{3,2,1,0:T(8,128)S(1)} collective-permute-done((f32[3,1,64,128]{3,2,1,0:T(8,128)S(1)}, f32[3,1,64,128]{3,2,1,0:T(8,128)S(1)}, u32[]{:S(2)}, u32[]{:S(2)}) %collective-permute-start.5) | collective-permute-done | bytes 98336 | tf_op jit(solution)/shard_map/ppermute | solution.py:18
  139.4 3.4 %multiply_reduce_fusion = f32[8,32,128,20]{2,1,0,3:T(8,128)S(1)} fusion(f32[8,32,128,3]{2,1,0,3:T(8,128)S(1)} %add_bitcast_fusion, bf16[20,3,8,32,128]{4,3,2,1,0:T(8,128)(2,1)} %param.9), kind=kLoop, calls=%fused_computation.2 | loop fusion | flops 5242880 | bytes 6946816 | tf_op jit(solution)/shard_map/kvyxl,vyxl->kyxl/dot_general | solution.py:105
  142.9 3.4 %collective-permute-start.6 = (f32[20,2,32,128]{3,2,1,0:T(8,128)S(1)}, f32[20,2,32,128]{3,2,1,0:T(8,128)S(1)}, u32[]{:S(2)}, u32[]{:S(2)}) collective-permute-start(f32[20,2,32,128]{3,2,1,0:T(8,128)S(1)} %get-tuple-element.9), channel_id=1, source_target_pairs={{0,1},{1,2},{2,3},{3,4},{4,5},{5,6},{6,7},{8,9},{9,10},{10,11},{11... | collective-permute-start | bytes 1966088 | tf_op jit(solution)/shard_map/ppermute | solution.py:15
  146.3 2.7 %collective-permute-start.7 = (f32[20,2,32,128]{3,2,1,0:T(8,128)S(1)}, f32[20,2,32,128]{3,2,1,0:T(8,128)S(1)}, u32[]{:S(2)}, u32[]{:S(2)}) collective-permute-start(f32[20,2,32,128]{3,2,1,0:T(8,128)S(1)} %get-tuple-element.10), channel_id=1, source_target_pairs={{1,0},{2,1},{3,2},{4,3},{5,4},{6,5},{7,6},{9,8},{10,9},{11,10},{12... | collective-permute-start | bytes 1966088 | tf_op jit(solution)/shard_map/ppermute | solution.py:18
  149.0 23.0 %collective-permute-done.6 = f32[20,2,32,128]{3,2,1,0:T(8,128)S(1)} collective-permute-done((f32[20,2,32,128]{3,2,1,0:T(8,128)S(1)}, f32[20,2,32,128]{3,2,1,0:T(8,128)S(1)}, u32[]{:S(2)}, u32[]{:S(2)}) %collective-permute-start.6) | collective-permute-done | bytes 655392 | tf_op jit(solution)/shard_map/ppermute | solution.py:15
  175.7 3.6 %convert_add_fusion = f32[20,8,32,128]{3,2,1,0:T(8,128)} fusion(bf16[20,8,32,128]{3,2,1,0:T(8,128)(2,1)S(1)} %copy-done.2, f32[20,12,32,128]{3,2,1,0:T(8,128)S(1)} %fusion.14, pred[12]{0:T(512)(128)(4,1)S(1)} %compare_and_fusion, bf16[128,128]{1,0:T(8,128)(2,1)S(1)} %copy-done), kind=kOutput, calls=%fused_computation.62 | convolution fusion | flops 1013841920 | bytes 7897100 | tf_op jit(solution)/shard_map/dot_general | solution.py:107
  (53 shorter events, 14.0 us)
Async XLA Ops:
  6.5 0.8 copy-start
  6.5 9.5 %copy-start.4 = (s32[1,2048]{1,0:T(1,128)S(1)}, s32[1,2048]{1,0:T(1,128)}, u32[]{:S(2)}) copy-start(s32[1,2048]{1,0:T(1,128)} %param.11) | copy-start | bytes 24580
  6.5 80.2 %all-reduce.12.cloned.1.call-start = ((), (), s32[]{:S(2)}) async-start(), calls=%async_computation | async-start | bytes 786432 | tf_op jit(solution)/shard_map/psum | solution.py:80
  10.1 32.7 %collective-permute-start = (f32[20,2,32,128]{3,2,1,0:T(8,128)}, f32[20,2,32,128]{3,2,1,0:T(8,128)}, u32[]{:S(2)}, u32[]{:S(2)}) collective-permute-start(f32[20,2,32,128]{3,2,1,0:T(8,128)} %get-tuple-element.11), channel_id=1, source_target_pairs={{0,1},{1,2},{2,3},{3,4},{4,5},{5,6},{6,7},{8,9},{9,10},{10,11},{11... | collective-permute-start | bytes 1966088 | tf_op jit(solution)/shard_map/ppermute | solution.py:15
  13.5 29.3 %collective-permute-start.1 = (f32[20,2,32,128]{3,2,1,0:T(8,128)S(1)}, f32[20,2,32,128]{3,2,1,0:T(8,128)}, u32[]{:S(2)}, u32[]{:S(2)}) collective-permute-start(f32[20,2,32,128]{3,2,1,0:T(8,128)S(1)} %get-tuple-element.12), channel_id=1, source_target_pairs={{1,0},{2,1},{3,2},{4,3},{5,4},{6,5},{7,6},{9,8},{10,9},{11,10},{12... | collective-permute-start | bytes 1966088 | tf_op jit(solution)/shard_map/ppermute | solution.py:18
  48.9 2.1 %copy-start.1 = (bf16[20,3,8,32,128]{4,3,2,1,0:T(8,128)(2,1)S(1)}, bf16[20,3,8,32,128]{4,3,2,1,0:T(8,128)(2,1)}, u32[]{:S(2)}) copy-start(bf16[20,3,8,32,128]{4,3,2,1,0:T(8,128)(2,1)} %param.9) | copy-start | bytes 11796484
  51.0 1.7 copy-start.8
  51.0 1.8 copy-start.7
  87.6 6.7 %collective-permute-start.2 = (f32[3,1,32,128]{3,2,1,0:T(8,128)S(1)}, f32[3,1,32,128]{3,2,1,0:T(8,128)S(1)}, u32[]{:S(2)}, u32[]{:S(2)}) collective-permute-start(f32[3,1,32,128]{3,2,1,0:T(8,128)S(1)} %get-tuple-element.19), channel_id=1, source_target_pairs={{0,1},{1,2},{2,3},{3,4},{4,5},{5,6},{6,7},{8,9},{9,10},{10,11},{11... | collective-permute-start | bytes 147464 | tf_op jit(solution)/shard_map/ppermute | solution.py:15
  90.9 6.9 %collective-permute-start.3 = (f32[3,1,32,128]{3,2,1,0:T(8,128)S(1)}, f32[3,1,32,128]{3,2,1,0:T(8,128)S(1)}, u32[]{:S(2)}, u32[]{:S(2)}) collective-permute-start(f32[3,1,32,128]{3,2,1,0:T(8,128)S(1)} %get-tuple-element.20), channel_id=1, source_target_pairs={{1,0},{2,1},{3,2},{4,3},{5,4},{6,5},{7,6},{9,8},{10,9},{11,10},{12... | collective-permute-start | bytes 147464 | tf_op jit(solution)/shard_map/ppermute | solution.py:18
  101.1 13.1 %copy-start.3 = (s32[1,2048]{1,0:T(1,128)S(1)}, s32[1,2048]{1,0:T(1,128)}, u32[]{:S(2)}) copy-start(s32[1,2048]{1,0:T(1,128)} %param.12) | copy-start | bytes 24580
  101.1 13.7 %copy-start.5 = (f32[1,2048]{1,0:T(1,128)S(1)}, f32[1,2048]{1,0:T(1,128)}, u32[]{:S(2)}) copy-start(f32[1,2048]{1,0:T(1,128)} %param.15) | copy-start | bytes 24580
  101.1 13.7 %copy-start.6 = (f32[1,2048]{1,0:T(1,128)S(1)}, f32[1,2048]{1,0:T(1,128)}, u32[]{:S(2)}) copy-start(f32[1,2048]{1,0:T(1,128)} %param.14) | copy-start | bytes 24580
  128.0 7.5 %collective-permute-start.4 = (f32[3,1,64,128]{3,2,1,0:T(8,128)S(1)}, f32[3,1,64,128]{3,2,1,0:T(8,128)S(1)}, u32[]{:S(2)}, u32[]{:S(2)}) collective-permute-start(f32[3,1,64,128]{3,2,1,0:T(8,128)S(1)} %get-tuple-element.13), channel_id=1, source_target_pairs={{0,1},{1,2},{2,3},{3,4},{4,5},{5,6},{6,7},{8,9},{9,10},{10,11},{11... | collective-permute-start | bytes 294920 | tf_op jit(solution)/shard_map/ppermute | solution.py:15
  130.5 7.4 %collective-permute-start.5 = (f32[3,1,64,128]{3,2,1,0:T(8,128)S(1)}, f32[3,1,64,128]{3,2,1,0:T(8,128)S(1)}, u32[]{:S(2)}, u32[]{:S(2)}) collective-permute-start(f32[3,1,64,128]{3,2,1,0:T(8,128)S(1)} %get-tuple-element.14), channel_id=1, source_target_pairs={{1,0},{2,1},{3,2},{4,3},{5,4},{6,5},{7,6},{9,8},{10,9},{11,10},{12... | collective-permute-start | bytes 294920 | tf_op jit(solution)/shard_map/ppermute | solution.py:18
  142.9 29.1 %collective-permute-start.6 = (f32[20,2,32,128]{3,2,1,0:T(8,128)S(1)}, f32[20,2,32,128]{3,2,1,0:T(8,128)S(1)}, u32[]{:S(2)}, u32[]{:S(2)}) collective-permute-start(f32[20,2,32,128]{3,2,1,0:T(8,128)S(1)} %get-tuple-element.9), channel_id=1, source_target_pairs={{0,1},{1,2},{2,3},{3,4},{4,5},{5,6},{6,7},{8,9},{9,10},{10,11},{11... | collective-permute-start | bytes 1966088 | tf_op jit(solution)/shard_map/ppermute | solution.py:15
  146.3 25.7 %collective-permute-start.7 = (f32[20,2,32,128]{3,2,1,0:T(8,128)S(1)}, f32[20,2,32,128]{3,2,1,0:T(8,128)S(1)}, u32[]{:S(2)}, u32[]{:S(2)}) collective-permute-start(f32[20,2,32,128]{3,2,1,0:T(8,128)S(1)} %get-tuple-element.10), channel_id=1, source_target_pairs={{1,0},{2,1},{3,2},{4,3},{5,4},{6,5},{7,6},{9,8},{10,9},{11,10},{12... | collective-permute-start | bytes 1966088 | tf_op jit(solution)/shard_map/ppermute | solution.py:18
  174.3 1.3 copy-start.2
Sparse Core Ops, SparseCore 0:
  52.8 33.8 all-reduce.11
where the time goes:
time: 188 us; the launch traced here: 186 us
  waiting for transfers between devices  91.1 us (48%)
  other arithmetic  31.5 us (17%)
  starting transfers between devices  23.8 us (13%)
  local copies, waits for them, and re-layouts  19.9 us (11%)
  between operations  14.4 us (8%)
  matrix products  5.39 us (3%)
    ppermute x4, waiting for transfers between devices, padded_2(): lax.ppermute(lax.slice_in_dim(block, block.shape[dim] - width, None, axis...  51.4 us
    psum x1, waiting for transfers between devices, on_device(): increment = lax.psum(partial_inc, 'mem')  33.8 us
    unnamed x6, other arithmetic  14.7 us
    gather x1, local copies, waits for them, and re-layouts, on_device(): picked = flat[variable, column]  13 us
    ppermute x4, starting transfers between devices, padded_2(): lax.ppermute(lax.slice_in_dim(block, block.shape[dim] - width, None, axis...  12.6 us
    ppermute x4, starting transfers between devices, padded_2(): lax.ppermute(lax.slice_in_dim(block, 0, width, axis=dim), axis, backward)  11.1 us
    ppermute x4, waiting for transfers between devices, padded_2(): lax.ppermute(lax.slice_in_dim(block, 0, width, axis=dim), axis, backward)  5.94 us
  transfers between devices with their start and end apart: 9, of which 6 were waited for; matrix products, arithmetic and copies ran while one was open for 0% of the time, Pallas kernels for 0%

commit v1 on v0

v1 whole, which is shorter than its diff:
```python
import functools

import jax
import jax.numpy as jnp
from jax import lax
from jax.experimental import pallas as pl
from jax.experimental.pallas import tpu as pltpu
from jax.sharding import PartitionSpec as P

V = 3
F32 = jnp.float32
BF16 = jnp.bfloat16
MESH = pl.DeviceIdType.MESH


def split2(x):
    hi = x.astype(BF16)
    lo = (x - hi.astype(F32)).astype(BF16)
    return hi, lo


def dot(a, b):
    return jnp.dot(a, b, preferred_element_type=F32)


def dot_nt(a, b):
    return lax.dot_general(a, b, (((1,), (1,)), ((), ())), preferred_element_type=F32)


def band(distance):
    d = jnp.abs(distance)
    return jnp.where(d == 0, 6.0, jnp.where(d == 1, 4.0, jnp.where(d == 2, 1.0, 0.0)))


def column_weight(c, c2, cols):
    end = (c == c2) & ((c == 0) | (c == cols - 1))
    return (band(c - c2) - jnp.where(end, 1.0, 0.0)) * (1.0 / 16.0)


def kernel(n, tiles, chunks, alpha, ens_hbm, loc, col, lev, cnt, innov, wgt, out,
           ens, hs, hr, gs, gr, lbe, mm, em, wt, inci, ince, reci, rece, redi, rede,
           incf, incg, ihalo, adj, adjs, ahalo,
           ens_sem, hs_sem, hr_sem, gs_sem, gr_sem, rs_s, rs_r, ag_s, ag_r, ih_s, ih_r, ah_s, ah_r):
    members, rows, cols, levels = alpha.shape
    size = rows * cols
    cq = cols // n
    per = members // chunks
    m = lax.axis_index("mem")
    t = lax.axis_index("tile")
    has = (t > 0, t < tiles - 1)
    near = (t - 1, t + 1)
    ens_copy = pltpu.make_async_copy(ens_hbm, ens, ens_sem)
    ens_copy.start()

    barrier = pltpu.get_barrier_semaphore()
    for d in range(1, n):
        pl.semaphore_signal(barrier, inc=1, device_id={"mem": lax.rem(m + d, n), "tile": t}, device_id_type=MESH)
    for s in range(2):
        @pl.when(has[s])
        def _(s=s):
            pl.semaphore_signal(barrier, inc=1, device_id={"mem": m, "tile": near[s]}, device_id_type=MESH)

    hs[0] = alpha[:, 0:2].astype(F32)
    hs[1] = alpha[:, rows - 2 : rows].astype(F32)
    pl.semaphore_wait(barrier, n - 1 + has[0].astype(jnp.int32) + has[1].astype(jnp.int32))

    def halo(src, dst, ssem, rsem, s):
        return pltpu.make_async_remote_copy(
            src_ref=src, dst_ref=dst, send_sem=ssem, recv_sem=rsem,
            device_id={"mem": m, "tile": near[s]}, device_id_type=MESH)

    def edge_copy(src, dst, ssem, rsem, s, c):
        part = pl.ds(c * per, per)
        return halo(src.at[s, part], dst.at[1 - s, part], ssem.at[s, c], rsem.at[1 - s, c], s)

    for c in range(chunks):
        for s in range(2):
            @pl.when(has[s])
            def _(s=s, c=c):
                edge_copy(hs, hr, hs_sem, hr_sem, s, c).start()
    for s in range(2):
        @pl.when(jnp.logical_not(has[s]))
        def _(s=s):
            hr[s] = jnp.zeros(hr.shape[1:], F32)
            gr[s] = jnp.zeros(gr.shape[1:], F32)
            ihalo[s] = jnp.zeros(ihalo.shape[1:], F32)
            ahalo[s] = jnp.zeros(ahalo.shape[1:], F32)

    i = lax.broadcasted_iota(jnp.int32, (size, size), 0)
    j = lax.broadcasted_iota(jnp.int32, (size, size), 1)
    r, r2 = lax.div(i, cols), lax.div(j, cols)
    end = (r == r2) & (((r == 0) & (t == 0)) | ((r == rows - 1) & (t == tiles - 1)))
    row_weight = (band(r - r2) - jnp.where(end, 1.0, 0.0)) * (1.0 / 16.0)
    mm[...] = (row_weight * column_weight(i - r * cols, j - r2 * cols, cols)).astype(BF16)
    i = lax.broadcasted_iota(jnp.int32, (4 * cols, 4 * cols), 0)
    j = lax.broadcasted_iota(jnp.int32, (4 * cols, 4 * cols), 1)
    q, q2 = lax.div(i, cols), lax.div(j, cols)
    r = jnp.where(q < 2, q, q + rows - 4)
    r2 = jnp.where(q2 < 2, q2 - 2, q2 - 2 + rows)
    em[...] = (band(r - r2) * (1.0 / 16.0) * column_weight(i - q * cols, j - q2 * cols, cols)).astype(BF16)

    inci[...] = jnp.zeros_like(inci)
    ince[...] = jnp.zeros_like(ince)
    ens_copy.wait()
    lv = loc[...]

    def lift(k, carry):
        hi, lo = split2(dot(mm[...], alpha[k].reshape(size, levels)))
        base = (dot_nt(hi, lv) + dot_nt(lo, lv)).reshape(rows, cols, levels)
        lbe[k, 0:2] = base[0:2]
        lbe[k, 2:4] = base[rows - 2 : rows]
        inner = base[2 : rows - 2].astype(BF16).astype(F32)
        for v in range(V):
            inci[v] += ens[k, v, 2 : rows - 2].astype(F32) * inner
        return carry

    lax.fori_loop(0, members, lift, 0)

    def spread_copy(part, rec, d, which):
        peer = lax.rem(m + d, n)
        return pltpu.make_async_remote_copy(
            src_ref=part.at[:, :, pl.ds(pl.multiple_of(peer * cq, cq), cq), :], dst_ref=rec.at[d - 1],
            send_sem=rs_s.at[which, d - 1], recv_sem=rs_r.at[which, d - 1],
            device_id={"mem": peer, "tile": t}, device_id_type=MESH)

    def gather_copy(red, full, d, which):
        peer = lax.rem(m + d, n)
        return pltpu.make_async_remote_copy(
            src_ref=red, dst_ref=full.at[:, :, pl.ds(pl.multiple_of(m * cq, cq), cq), :],
            send_sem=ag_s.at[which, d - 1], recv_sem=ag_r.at[which, d - 1],
            device_id={"mem": peer, "tile": t}, device_id_type=MESH)

    def reduce(part, rec, red, full, which):
        mine = pl.ds(pl.multiple_of(m * cq, cq), cq)
        for d in range(1, n):
            spread_copy(part, rec, d, which).start()
        total = part[:, :, mine, :]
        for d in range(1, n):
            spread_copy(part, rec, d, which).wait_recv()
            total = total + rec[d - 1]
        red[...] = total
        for d in range(1, n):
            gather_copy(red, full, d, which).start()
        full[:, :, mine, :] = total

    def finish(part, rec, red, full, which):
        for d in range(1, n):
            gather_copy(red, full, d, which).wait_recv()
        for d in range(1, n):
            spread_copy(part, rec, d, which).wait_send()
            gather_copy(red, full, d, which).wait_send()

    reduce(inci, reci, redi, incf, 0)

    slots = col.shape[1]
    place = col[...]
    wide = 2 * cols
    frow = lax.div(place, wide)
    fcol = place - frow * wide
    slot = lax.broadcasted_iota(jnp.int32, (1, slots), 1)
    variable = lax.rem(slot, V)

    def weights(fine, count, shift):
        main = lax.div(fine, 2)
        other = jnp.where(fine - 2 * main == 1, main + 1, main - 1)
        at = lax.broadcasted_iota(jnp.int32, (count, slots), 0) - shift
        return jnp.where(at == main, 0.75, 0.0) + jnp.where(at == other, 0.25, 0.0)

    wr = weights(frow, rows + 2, 1)
    wc = weights(fcol, cols, 0)
    for v in range(V):
        mask = jnp.where(variable == v, 1.0, 0.0)
        for a in range(rows + 2):
            start = (v * (rows + 2) + a) * cols
            wt[start : start + cols, :] = (wc * (wr[a : a + 1, :] * mask)).astype(BF16)
    finish(inci, reci, redi, incf, 0)

    for c in range(chunks):
        for s in range(2):
            @pl.when(has[s])
            def _(s=s, c=c):
                part = pl.ds(c * per, per)
                halo(hs.at[s, part], hr.at[s, part], hs_sem.at[s, c], hr_sem.at[s, c], s).wait_recv()

        def lift_edge(k, carry):
            around = jnp.concatenate([hr[0, k], hr[1, k]], axis=0).astype(BF16).reshape(4 * cols, levels)
            hi, lo = split2(dot(em[...], around))
            edge = (dot_nt(hi, lv) + dot_nt(lo, lv)).reshape(4, cols, levels) + lbe[k]
            edge = edge.astype(BF16).astype(F32)
            for v in range(V):
                ince[v, 0:2] += ens[k, v, 0:2].astype(F32) * edge[0:2]
                ince[v, 2:4] += ens[k, v, rows - 2 : rows].astype(F32) * edge[2:4]
            return carry

        lax.fori_loop(c * per, (c + 1) * per, lift_edge, 0)

    reduce(ince, rece, rede, incg, 1)
    finish(ince, rece, rede, incg, 1)

    def ihalo_copy(s):
        return halo(incg.at[:, 3 * s], ihalo.at[1 - s], ih_s.at[s], ih_r.at[1 - s], s)

    def ihalo_wait(s):
        return halo(incg.at[:, 3 * s], ihalo.at[s], ih_s.at[s], ih_r.at[s], s)

    for s in range(2):
        @pl.when(has[s])
        def _(s=s):
            ihalo_copy(s).start()
    for s in range(2):
        @pl.when(has[s])
        def _(s=s):
            ihalo_wait(s).wait_recv()
            ihalo_copy(s).wait_send()

    places = V * (rows + 2) * cols
    whole = jnp.concatenate(
        [ihalo[0][:, None], incg[:, 0:2], incf[...], incg[:, 2:4], ihalo[1][:, None]], axis=1
    ).reshape(places, levels)
    flipped = whole.T
    hi, lo = split2(flipped)
    picked = dot(hi, wt[...]) + dot(lo, wt[...])
    hot = lax.broadcasted_iota(jnp.int32, (levels, slots), 0) == lev[...]
    value = jnp.sum(jnp.where(hot, picked, 0.0), axis=0, keepdims=True)
    weighted = jnp.where(slot < cnt[0], wgt[...] * (value - innov[...]), 0.0)
    sent = jnp.where(hot, jnp.broadcast_to(weighted, hot.shape), 0.0)
    hi, lo = split2(sent)
    adjoint = (dot_nt(wt[...], hi) + dot_nt(wt[...], lo)).reshape(V, rows + 2, cols, levels)
    adjs[0] = adjoint[:, 0]
    adjs[1] = adjoint[:, rows + 1]

    def ahalo_copy(s, slot_there):
        return halo(adjs.at[s], ahalo.at[slot_there], ah_s.at[s], ah_r.at[slot_there], s)

    for s in range(2):
        @pl.when(has[s])
        def _(s=s):
            ahalo_copy(s, 1 - s).start()
    adj[...] = adjoint[:, 1 : rows + 1]
    for s in range(2):
        @pl.when(has[s])
        def _(s=s):
            ahalo_copy(s, s).wait_recv()
            ahalo_copy(s, 1 - s).wait_send()
    adj[:, 0] += ahalo[0]
    adj[:, rows - 1] += ahalo[1]

    def field(k, low, high):
        total = ens[k, 0, low:high].astype(F32) * adj[0, low:high]
        for v in range(1, V):
            total = total + ens[k, v, low:high].astype(F32) * adj[v, low:high]
        return total

    for c in range(chunks):
        def edges(k, carry):
            gs[0, k] = field(k, 0, 2)
            gs[1, k] = field(k, rows - 2, rows)
            return carry

        lax.fori_loop(c * per, (c + 1) * per, edges, 0)
        for s in range(2):
            @pl.when(has[s])
            def _(s=s, c=c):
                edge_copy(gs, gr, gs_sem, gr_sem, s, c).start()

    def raised(x):
        hi, lo = split2(x)
        return split2(dot(hi, lv) + dot(lo, lv))

    def inside(k, carry):
        g = jnp.concatenate([gs[0, k], field(k, 2, rows - 2), gs[1, k]], axis=0).reshape(size, levels)
        hi, lo = raised(g)
        back = dot(mm[...], hi) + dot(mm[...], lo)
        out[k] = alpha[k].astype(F32) + back.reshape(rows, cols, levels)
        return carry

    lax.fori_loop(0, members, inside, 0)

    for c in range(chunks):
        for s in range(2):
            @pl.when(has[s])
            def _(s=s, c=c):
                part = pl.ds(c * per, per)
                halo(gs.at[s, part], gr.at[s, part], gs_sem.at[s, c], gr_sem.at[s, c], s).wait_recv()

        def outer(k, carry):
            around = jnp.concatenate([gr[0, k], gr[1, k]], axis=0).reshape(4 * cols, levels)
            hi, lo = raised(around)
            back = (dot(em[...], hi) + dot(em[...], lo)).reshape(4, cols, levels)
            out[k, 0:2] += back[0:2]
            out[k, rows - 2 : rows] += back[2:4]
            return carry

        lax.fori_loop(c * per, (c + 1) * per, outer, 0)
    for c in range(chunks):
        for s in range(2):
            @pl.when(has[s])
            def _(s=s, c=c):
                edge_copy(hs, hr, hs_sem, hr_sem, s, c).wait_send()
                edge_copy(gs, gr, gs_sem, gr_sem, s, c).wait_send()


def solution(mesh):
    n = mesh.shape["mem"]
    tiles = mesh.shape["tile"]

    def on_device(alpha, ensemble, loc_vert, obs_col, obs_lev, obs_count, innovation, obs_weight):
        members, rows, cols, levels = alpha.shape
        slots = obs_col.shape[1]
        chunks = 4 if members % 4 == 0 else 1
        cq = cols // n
        vmem = pl.BlockSpec(memory_space=pltpu.VMEM)
        edge = pltpu.VMEM((2, members, 2, cols, levels), F32)
        dma = pltpu.SemaphoreType.DMA
        return pl.pallas_call(
            functools.partial(kernel, n, tiles, chunks),
            out_shape=jax.ShapeDtypeStruct(alpha.shape, F32),
            in_specs=[vmem, pl.BlockSpec(memory_space=pl.ANY), vmem, vmem, vmem,
                      pl.BlockSpec(memory_space=pltpu.SMEM), vmem, vmem],
            out_specs=vmem,
            scratch_shapes=[
                pltpu.VMEM(ensemble.shape, BF16), edge, edge, edge, edge,
                pltpu.VMEM((members, 4, cols, levels), F32),
                pltpu.VMEM((rows * cols, rows * cols), BF16),
                pltpu.VMEM((4 * cols, 4 * cols), BF16),
                pltpu.VMEM((V * (rows + 2) * cols, slots), BF16),
                pltpu.VMEM((V, rows - 4, cols, levels), F32),
                pltpu.VMEM((V, 4, cols, levels), F32),
                pltpu.VMEM((n - 1, V, rows - 4, cq, levels), F32),
                pltpu.VMEM((n - 1, V, 4, cq, levels), F32),
                pltpu.VMEM((V, rows - 4, cq, levels), F32),
                pltpu.VMEM((V, 4, cq, levels), F32),
                pltpu.VMEM((V, rows - 4, cols, levels), F32),
                pltpu.VMEM((V, 4, cols, levels), F32),
                pltpu.VMEM((2, V, cols, levels), F32),
                pltpu.VMEM((V, rows, cols, levels), F32),
                pltpu.VMEM((2, V, cols, levels), F32),
                pltpu.VMEM((2, V, cols, levels), F32),
                dma, dma((2, chunks)), dma((2, chunks)), dma((2, chunks)), dma((2, chunks)),
                dma((2, n - 1)), dma((2, n - 1)), dma((2, n - 1)), dma((2, n - 1)),
                dma((2,)), dma((2,)), dma((2,)), dma((2,)),
            ],
            compiler_params=pltpu.CompilerParams(
                collective_id=0, has_side_effects=True, vmem_limit_bytes=60 << 20),
        )(alpha, ensemble, loc_vert, obs_col, obs_lev, obs_count, innovation, obs_weight)

    in_specs = (
        P("mem", "tile", None, None),
        P("mem", None, "tile", None, None),
        P(),
        P("tile", None),
        P("tile", None),
        P("tile"),
        P("tile", None),
        P("tile", None),
    )
    out_specs = P("mem", "tile", None, None)
    return jax.shard_map(
        on_device, mesh=mesh, in_specs=in_specs, out_specs=out_specs, check_vma=False
    )
```

time: 188 us -> 91.2 us (0.49)
  waiting for transfers between devices: 91.1 us -> 0 us
  Pallas kernels: 0 us -> 86.8 us
  other arithmetic: 31.5 us -> 0 us
  starting transfers between devices: 23.8 us -> 0 us
  local copies, waits for them, and re-layouts: 19.9 us -> 3.57 us
  between operations: 14.4 us -> 0.66 us
  matrix products: 5.39 us -> 0 us
    pallas_call x0 -> x1, Pallas kernels: none -> 86.8 us  [on_device(): pl.pallas_call(functools.partial(kernel, n, tiles, chunks), out_shape=jax...]
    ppermute x8 -> x0, waiting for transfers between devices: 57.3 us -> none  [the longest x4 51.4 us: padded_2(): lax.ppermute(lax.slice_in_dim(block, block.shape[dim] - width, None, axis...]
    psum x1 -> x0, waiting for transfers between devices: 33.8 us -> none  [on_device(): increment = lax.psum(partial_inc, 'mem')]
    ppermute x8 -> x0, starting transfers between devices: 23.8 us -> none  [the longest x4 12.6 us: padded_2(): lax.ppermute(lax.slice_in_dim(block, block.shape[dim] - width, None, axis...]
    unnamed x6 -> x0, other arithmetic: 14.7 us -> none
    gather x1 -> x0, local copies, waits for them, and re-layouts: 13 us -> none  [on_device(): picked = flat[variable, column]]
    dot_general x2 -> x0, matrix products: 5.39 us -> none  [the longest x1 3.58 us: on_device(): jnp.dot(back, loc_vert.astype(jnp.float32), precision=lax.Precision.HIGHEST)]
    dot_general x2 -> x0, other arithmetic: 5.07 us -> none  [the longest x1 3.38 us: on_device(): jnp.einsum('kvyxl,vyxl->kyxl', ensemble.astype(jnp.float32), coarse_adjoint)]
  transfers between devices with their start and end apart: 9 -> 0, of which waited for: 6 -> 0; matrix products, arithmetic and copies ran while one was open for 0% -> 0% of each run, Pallas kernels for 0% -> 0%
where the time goes in v1:
time: 91.2 us; the launch traced here: 91 us
  Pallas kernels  86.8 us (95%)
  local copies, waits for them, and re-layouts  3.57 us (4%)
    pallas_call x1, Pallas kernels, on_device(): pl.pallas_call(functools.partial(kernel, n, tiles, chunks), out_shape=jax...  86.8 us
    unnamed x1, local copies, waits for them, and re-layouts  3.57 us

profile of v1, /device:TPU:12, one launch (start us, length us, event | category | flops | bytes accessed | tf_op | source)
XLA Modules:
  0.0 91.0 jit_solution(762360556773811989)
XLA Ops:
  0.7 86.8 %shard_map.82 = f32[20,8,32,128]{3,2,1,0:T(8,128)} custom-call(bf16[20,8,32,128]{3,2,1,0:T(8,128)(2,1)} %alpha.1, bf16[20,3,8,32,128]{4,3,2,1,0:T(8,128)(2,1)} %ens_hbm.1, bf16[128,128]{1,0:T(8,128)(2,1)} %loc.1, s32[1,2048]{1,0:T(1,128)} %col.1, s32[1,2048]{1,0:T(1,128)} %lev.1, s32[1]{0:T(128)S(6)} %copy.10.cnt, f32[1,2048]{1,0:T(1,128)} %innov.1, ...), custom_call_target="tpu_custom_call" | custom-call | tf_op jit(solution)/shard_map/pallas_call | solution.py:315
  87.4 3.6 %copy.11 = f32[20,8,32,128]{3,2,1,0:T(8,128)} copy(f32[20,8,32,128]{3,2,1,0:T(8,128)} %shard_map.82) | data formatting | bytes 5242880

commit v2 on v1

--- a/solution.py
+++ b/solution.py
@@ -58,11 +58,12 @@
     for s in range(2):
         @pl.when(has[s])
         def _(s=s):
-            pl.semaphore_signal(barrier, inc=1, device_id={"mem": m, "tile": near[s]}, device_id_type=MESH)
+            for d in range(n):
+                pl.semaphore_signal(barrier, inc=1, device_id={"mem": lax.rem(m + d, n), "tile": near[s]}, device_id_type=MESH)
 
     hs[0] = alpha[:, 0:2].astype(F32)
     hs[1] = alpha[:, rows - 2 : rows].astype(F32)
-    pl.semaphore_wait(barrier, n - 1 + has[0].astype(jnp.int32) + has[1].astype(jnp.int32))
+    pl.semaphore_wait(barrier, n - 1 + n * (has[0].astype(jnp.int32) + has[1].astype(jnp.int32)))
 
     def halo(src, dst, ssem, rsem, s):
         return pltpu.make_async_remote_copy(
@@ -130,6 +131,12 @@
             send_sem=ag_s.at[which, d - 1], recv_sem=ag_r.at[which, d - 1],
             device_id={"mem": peer, "tile": t}, device_id_type=MESH)
 
+    def ihalo_copy(s, slot, d):
+        return pltpu.make_async_remote_copy(
+            src_ref=rede.at[:, 3 * s], dst_ref=ihalo.at[slot, :, pl.ds(pl.multiple_of(m * cq, cq), cq), :],
+            send_sem=ih_s.at[s, d], recv_sem=ih_r.at[slot, d],
+            device_id={"mem": lax.rem(m + d, n), "tile": near[s]}, device_id_type=MESH)
+
     def reduce(part, rec, red, full, which):
         mine = pl.ds(pl.multiple_of(m * cq, cq), cq)
         for d in range(1, n):
@@ -139,6 +146,12 @@
             spread_copy(part, rec, d, which).wait_recv()
             total = total + rec[d - 1]
         red[...] = total
+        if which == 1:
+            for s in range(2):
+                @pl.when(has[s])
+                def _(s=s):
+                    for d in range(n):
+                        ihalo_copy(s, 1 - s, d).start()
         for d in range(1, n):
             gather_copy(red, full, d, which).start()
         full[:, :, mine, :] = total
@@ -171,7 +184,7 @@
     for v in range(V):
         mask = jnp.where(variable == v, 1.0, 0.0)
         for a in range(rows + 2):
-            start = (v * (rows + 2) + a) * cols
+            start = (a * V + v) * cols
             wt[start : start + cols, :] = (wc * (wr[a : a + 1, :] * mask)).astype(BF16)
     finish(inci, reci, redi, incf, 0)
 
@@ -197,26 +210,17 @@
     reduce(ince, rece, rede, incg, 1)
     finish(ince, rece, rede, incg, 1)
 
-    def ihalo_copy(s):
-        return halo(incg.at[:, 3 * s], ihalo.at[1 - s], ih_s.at[s], ih_r.at[1 - s], s)
-
-    def ihalo_wait(s):
-        return halo(incg.at[:, 3 * s], ihalo.at[s], ih_s.at[s], ih_r.at[s], s)
-
     for s in range(2):
         @pl.when(has[s])
         def _(s=s):
-            ihalo_copy(s).start()
-    for s in range(2):
-        @pl.when(has[s])
-        def _(s=s):
-            ihalo_wait(s).wait_recv()
-            ihalo_copy(s).wait_send()
+            for d in range(n):
+                ihalo_copy(s, s, d).wait_recv()
+                ihalo_copy(s, 1 - s, d).wait_send()
 
     places = V * (rows + 2) * cols
-    whole = jnp.concatenate(
-        [ihalo[0][:, None], incg[:, 0:2], incf[...], incg[:, 2:4], ihalo[1][:, None]], axis=1
-    ).reshape(places, levels)
+    pieces = [ihalo[0], incg[:, 0], incg[:, 1]] + [incf[:, a] for a in range(rows - 4)]
+    pieces += [incg[:, 2], incg[:, 3], ihalo[1]]
+    whole = jnp.concatenate(pieces, axis=0).reshape(places, levels)
     flipped = whole.T
     hi, lo = split2(flipped)
     picked = dot(hi, wt[...]) + dot(lo, wt[...])
@@ -225,9 +229,14 @@
     weighted = jnp.where(slot < cnt[0], wgt[...] * (value - innov[...]), 0.0)
     sent = jnp.where(hot, jnp.broadcast_to(weighted, hot.shape), 0.0)
     hi, lo = split2(sent)
-    adjoint = (dot_nt(wt[...], hi) + dot_nt(wt[...], lo)).reshape(V, rows + 2, cols, levels)
-    adjs[0] = adjoint[:, 0]
-    adjs[1] = adjoint[:, rows + 1]
+    sent2 = jnp.concatenate([hi, lo], axis=0)
+
+    def adjoint(a, count):
+        both = dot_nt(wt[a * V * cols : (a + count) * V * cols, :], sent2)
+        return (both[:, :levels] + both[:, levels:]).reshape(count, V, cols, levels)
+
+    adjs[0] = adjoint(0, 1)[0]
+    adjs[1] = adjoint(rows + 1, 1)[0]
 
     def ahalo_copy(s, slot_there):
         return halo(adjs.at[s], ahalo.at[slot_there], ah_s.at[s], ah_r.at[slot_there], s)
@@ -236,14 +245,10 @@
         @pl.when(has[s])
         def _(s=s):
             ahalo_copy(s, 1 - s).start()
-    adj[...] = adjoint[:, 1 : rows + 1]
-    for s in range(2):
-        @pl.when(has[s])
-        def _(s=s):
-            ahalo_copy(s, s).wait_recv()
-            ahalo_copy(s, 1 - s).wait_send()
-    adj[:, 0] += ahalo[0]
-    adj[:, rows - 1] += ahalo[1]
+    top, bottom = adjoint(1, 2), adjoint(rows - 1, 2)
+    for a in range(2):
+        adj[:, a] = top[a]
+        adj[:, rows - 2 + a] = bottom[a]
 
     def field(k, low, high):
         total = ens[k, 0, low:high].astype(F32) * adj[0, low:high]
@@ -251,24 +256,44 @@
             total = total + ens[k, v, low:high].astype(F32) * adj[v, low:high]
         return total
 
-    for c in range(chunks):
-        def edges(k, carry):
-            gs[0, k] = field(k, 0, 2)
-            gs[1, k] = field(k, rows - 2, rows)
-            return carry
-
-        lax.fori_loop(c * per, (c + 1) * per, edges, 0)
-        for s in range(2):
-            @pl.when(has[s])
-            def _(s=s, c=c):
-                edge_copy(gs, gr, gs_sem, gr_sem, s, c).start()
+    def back_copy(s, slot, w, c):
+        part = pl.ds(c * per, per)
+        return halo(gs.at[s, w, part], gr.at[slot, w, part], gs_sem.at[s, w, c], gr_sem.at[slot, w, c], s)
+
+    def send_row(w):
+        where = (1 - w, rows - 2 + w)
+        for c in range(chunks):
+            def edges(k, carry):
+                for s in range(2):
+                    gs[s, w, k] = field(k, where[s], where[s] + 1)[0]
+                return carry
+
+            lax.fori_loop(c * per, (c + 1) * per, edges, 0)
+            for s in range(2):
+                @pl.when(has[s])
+                def _(s=s, c=c):
+                    back_copy(s, 1 - s, w, c).start()
+
+    send_row(0)
+    for s in range(2):
+        @pl.when(has[s])
+        def _(s=s):
+            ahalo_copy(s, s).wait_recv()
+            ahalo_copy(s, 1 - s).wait_send()
+    adj[:, 0] += ahalo[0]
+    adj[:, rows - 1] += ahalo[1]
+    send_row(1)
+    inner = adjoint(3, rows - 4)
+    for a in range(rows - 4):
+        adj[:, 2 + a] = inner[a]
 
     def raised(x):
         hi, lo = split2(x)
         return split2(dot(hi, lv) + dot(lo, lv))
 
     def inside(k, carry):
-        g = jnp.concatenate([gs[0, k], field(k, 2, rows - 2), gs[1, k]], axis=0).reshape(size, levels)
+        middle = field(k, 2, rows - 2).reshape(size - 4 * cols, levels)
+        g = jnp.concatenate([gs[0, 1, k], gs[0, 0, k], middle, gs[1, 0, k], gs[1, 1, k]], axis=0)
         hi, lo = raised(g)
         back = dot(mm[...], hi) + dot(mm[...], lo)
         out[k] = alpha[k].astype(F32) + back.reshape(rows, cols, levels)
@@ -280,11 +305,11 @@
         for s in range(2):
             @pl.when(has[s])
             def _(s=s, c=c):
-                part = pl.ds(c * per, per)
-                halo(gs.at[s, part], gr.at[s, part], gs_sem.at[s, c], gr_sem.at[s, c], s).wait_recv()
+                for w in range(2):
+                    back_copy(s, s, w, c).wait_recv()
 
         def outer(k, carry):
-            around = jnp.concatenate([gr[0, k], gr[1, k]], axis=0).reshape(4 * cols, levels)
+            around = jnp.concatenate([gr[0, 0, k], gr[0, 1, k], gr[1, 1, k], gr[1, 0, k]], axis=0)
             hi, lo = raised(around)
             back = (dot(em[...], hi) + dot(em[...], lo)).reshape(4, cols, levels)
             out[k, 0:2] += back[0:2]
@@ -297,7 +322,8 @@
             @pl.when(has[s])
             def _(s=s, c=c):
                 edge_copy(hs, hr, hs_sem, hr_sem, s, c).wait_send()
-                edge_copy(gs, gr, gs_sem, gr_sem, s, c).wait_send()
+                for w in range(2):
+                    back_copy(s, 1 - s, w, c).wait_send()
 
 
 def solution(mesh):
@@ -311,6 +337,7 @@
         cq = cols // n
         vmem = pl.BlockSpec(memory_space=pltpu.VMEM)
         edge = pltpu.VMEM((2, members, 2, cols, levels), F32)
+        turned = pltpu.VMEM((2, 2, members, cols, levels), F32)
         dma = pltpu.SemaphoreType.DMA
         return pl.pallas_call(
             functools.partial(kernel, n, tiles, chunks),
@@ -319,7 +346,7 @@
                       pl.BlockSpec(memory_space=pltpu.SMEM), vmem, vmem],
             out_specs=vmem,
             scratch_shapes=[
-                pltpu.VMEM(ensemble.shape, BF16), edge, edge, edge, edge,
+                pltpu.VMEM(ensemble.shape, BF16), edge, edge, turned, turned,
                 pltpu.VMEM((members, 4, cols, levels), F32),
                 pltpu.VMEM((rows * cols, rows * cols), BF16),
                 pltpu.VMEM((4 * cols, 4 * cols), BF16),
@@ -336,12 +363,12 @@
                 pltpu.VMEM((V, rows, cols, levels), F32),
                 pltpu.VMEM((2, V, cols, levels), F32),
                 pltpu.VMEM((2, V, cols, levels), F32),
-                dma, dma((2, chunks)), dma((2, chunks)), dma((2, chunks)), dma((2, chunks)),
+                dma, dma((2, chunks)), dma((2, chunks)), dma((2, 2, chunks)), dma((2, 2, chunks)),
                 dma((2, n - 1)), dma((2, n - 1)), dma((2, n - 1)), dma((2, n - 1)),
-                dma((2,)), dma((2,)), dma((2,)), dma((2,)),
+                dma((2, n)), dma((2, n)), dma((2,)), dma((2,)),
             ],
             compiler_params=pltpu.CompilerParams(
-                collective_id=0, has_side_effects=True, vmem_limit_bytes=60 << 20),
+                collective_id=0, has_side_effects=True, vmem_limit_bytes=50 << 20),
         )(alpha, ensemble, loc_vert, obs_col, obs_lev, obs_count, innovation, obs_weight)
 
     in_specs = (

time: 91.2 us -> 88.1 us (0.966)
  Pallas kernels: 86.8 us -> 80.6 us
  local copies, waits for them, and re-layouts: 3.57 us -> 6.35 us
    pallas_call x1, Pallas kernels: 86.8 us -> 80.6 us  [on_device(): pl.pallas_call(functools.partial(kernel, n, tiles, chunks), out_shape=jax...]
    unnamed x1 -> x13, local copies, waits for them, and re-layouts: 3.57 us -> 6.35 us
where the time goes in v2:
time: 88.1 us; the launch traced here: 87.6 us
  Pallas kernels  80.6 us (91%)
  local copies, waits for them, and re-layouts  6.35 us (7%)
    pallas_call x1, Pallas kernels, on_device(): pl.pallas_call(functools.partial(kernel, n, tiles, chunks), out_shape=jax...  80.6 us
    unnamed x13, local copies, waits for them, and re-layouts  6.35 us

profile of v2, /device:TPU:12, one launch (start us, length us, event | category | flops | bytes accessed | tf_op | source)
XLA Modules:
  0.0 87.6 jit_solution(14663157178745655259)
XLA Ops:
  0.7 0.0 copy-start
  0.7 1.3 %copy-done = bf16[20,8,32,128]{3,2,1,0:T(8,128)(2,1)S(1)} copy-done((bf16[20,8,32,128]{3,2,1,0:T(8,128)(2,1)S(1)}, bf16[20,8,32,128]{3,2,1,0:T(8,128)(2,1)}, u32[]{:S(2)}) %copy-start) | copy-done | bytes 1310744
  2.0 0.0 copy-start.1
  2.0 0.8 copy-done.1
  2.7 0.0 copy-start.2
  2.7 0.7 copy-done.2
  3.4 0.0 copy-start.3
  3.4 0.7 copy-done.3
  4.1 0.0 copy-start.4
  4.1 0.7 copy-done.4
  4.8 0.0 copy-start.5
  4.8 0.7 copy-done.5
  5.5 80.6 %shard_map.82 = f32[20,8,32,128]{3,2,1,0:T(8,128)S(1)} custom-call(bf16[20,8,32,128]{3,2,1,0:T(8,128)(2,1)S(1)} %copy-done, bf16[20,3,8,32,128]{4,3,2,1,0:T(8,128)(2,1)} %ens_hbm.1, bf16[128,128]{1,0:T(8,128)(2,1)S(1)} %copy-done.1, s32[1,2048]{1,0:T(1,128)S(1)} %copy-done.2, s32[1,2048]{1,0:T(1,128)S(1)} %copy-done.3, s32[1]{0:T(128)S(6)} %copy.10.cnt, ...), custom_call_target="tpu_custom_call" | custom-call | tf_op jit(solution)/shard_map/pallas_call | solution.py:342
  86.1 1.5 %copy.11 = f32[20,8,32,128]{3,2,1,0:T(8,128)} copy(f32[20,8,32,128]{3,2,1,0:T(8,128)S(1)} %shard_map.82) | data formatting | bytes 5242880
Async XLA Ops:
  0.7 1.3 %copy-start = (bf16[20,8,32,128]{3,2,1,0:T(8,128)(2,1)S(1)}, bf16[20,8,32,128]{3,2,1,0:T(8,128)(2,1)}, u32[]{:S(2)}) copy-start(bf16[20,8,32,128]{3,2,1,0:T(8,128)(2,1)} %alpha.1) | copy-start | bytes 3932164
  2.0 0.8 copy-start.1
  2.7 0.7 copy-start.2
  3.4 0.7 copy-start.3
  4.1 0.7 copy-start.4
  4.8 0.7 copy-start.5
